TPU v7x, 32 devices: a whole 2x2x4 slice. The times are simulated.
32 devices in a mesh: ens: 2 (over core), ctx: 4 (over y, x), group: 4 (over z).
Axes of the slice: x: 2, y: 2, z: 4, core: 2. Of those that a mesh axis runs over, the one named last changes fastest.
Arguments:
- latents: bfloat16 [8, 1024, 512], P('ens', ('ctx', 'group')), parts along dimension 0, may hold values from -6 to 6
- rotary_rows: bfloat16 [8, 1024, 64], P('ens', ('ctx', 'group')), parts along dimension 0, may hold values from -6 to 6
- latent_gain: float32 [512], replicated, may hold values from 0.25 to 1.75
- key_up: bfloat16 [1024, 16, 128], P('ens', 'group'), parts along dimension 0, may hold values from -0.25 to 0.25
- value_up: bfloat16 [1024, 16, 128], P('ens', 'group'), parts along dimension 0, may hold values from -0.25 to 0.25
Outputs:
- stored_keys: bfloat16 [8, 16, 192, 1024], P(('ens', 'ctx'), 'group'), parts along dimension 0
- stored_values: bfloat16 [8, 1024, 16, 128], P(('ens', 'ctx'), None, 'group'), parts along dimension 0
There are 2 independent parts, one for each index of `ens`. A program takes and returns all parts, laid end to end along the dimension named above; an argument that names none is the same for every part. Nothing has to cross between parts.
All inputs are finite; a program needn't handle non-finite values.
Results may differ from a plain program's by a relative error of at most 0.0049.
Values may be sent and summed in bfloat16 or wider, within the bound.
A program may use at most 64 MiB of HBM per device.

v0:
```python
import functools

import jax
import jax.numpy as jnp
from jax import lax
from jax.experimental import pallas as pl
from jax.experimental.pallas import tpu as pltpu
from jax.sharding import PartitionSpec as P

MESH = pl.DeviceIdType.MESH
LANES = 128


def partner(me, step, count):
    if count & (count - 1):
        return lax.rem(me + step, count)
    total, bit = 0, 1
    while bit < count:
        total = total + bit * lax.rem(me // bit + step // bit, 2)
        bit *= 2
    return total


def kernel(
    seqs, planes, heads, rotary,
    lat, rot, gain_in, key_up, value_up, keys, values,
    stage, raw, mid, rot_stage, key_stage, value_stage,
    wide, key_w, value_w, mixed, gain,
    lat_sem, local_sem, got, mid_got, own_up, own_down, side, mid_side, up, down,
):
    c, g = lax.axis_index("ctx"), lax.axis_index("group")
    blk, latent = lat.shape[1:]
    slabs = latent // LANES
    tail = slabs * blk
    half = blk // 2
    per_unit = LANES // blk
    key_part = key_w.shape[0] // heads
    size = value_w.shape[1] // heads

    lat_loads = [
        pltpu.make_async_copy(
            lat.at[:, :, pl.ds(k * LANES, LANES)],
            stage.at[:, pl.ds(k * blk, blk), :],
            lat_sem.at[k],
        )
        for k in range(slabs)
    ]
    loads = [
        pltpu.make_async_copy(rot, rot_stage, local_sem.at[0]),
        pltpu.make_async_copy(key_up, key_stage, local_sem.at[1]),
        pltpu.make_async_copy(value_up, value_stage, local_sem.at[2]),
        pltpu.make_async_copy(gain_in, gain, local_sem.at[3]),
    ]
    loads[0].start()
    for load in lat_loads + loads[1:]:
        load.start()

    barrier = pltpu.get_barrier_semaphore()

    @pl.loop(1, seqs)
    def _(b):
        pl.semaphore_signal(
            barrier, inc=1, device_id={"ctx": partner(c, b, seqs)}, device_id_type=MESH
        )

    @pl.when(g > 0)
    def _():
        pl.semaphore_signal(barrier, inc=1, device_id={"group": g - 1}, device_id_type=MESH)

    @pl.when(g < planes - 1)
    def _():
        pl.semaphore_signal(barrier, inc=1, device_id={"group": g + 1}, device_id_type=MESH)

    loads[0].wait()

    @pl.loop(0, seqs)
    def _(s):
        block = rot_stage[s].astype(jnp.float32)
        both = jnp.concatenate([block[:half], block[half:]], axis=1)
        stage[s, pl.ds(tail, half), :] = both.astype(jnp.bfloat16)

    for load in lat_loads:
        load.wait()
    peers = seqs - 1 + jnp.minimum(g, 1) + jnp.minimum(planes - 1 - g, 1)
    pl.semaphore_wait(barrier, peers)

    def remote(src, dst, out_sem, in_sem, to):
        return pltpu.make_async_remote_copy(
            src_ref=src, dst_ref=dst, send_sem=out_sem, recv_sem=in_sem,
            device_id=to, device_id_type=MESH,
        )

    def own_out(s, way, out_sem, to):
        return remote(
            stage.at[s], mid.at[way, s], out_sem.at[s], mid_got.at[way, s], {"group": to}
        )

    def own_along(out_sem, to):
        return remote(stage.at[c], raw.at[c, g], out_sem.at[c], got.at[g, c], {"group": to})

    def own_side(s):
        return remote(stage.at[s], raw.at[c, g], side.at[s], got.at[g, c], {"ctx": s})

    def scatter(way, s, p):
        return remote(
            mid.at[way, s], raw.at[c, p], mid_side.at[way, s], got.at[p, c], {"ctx": s}
        )

    def relay(p, q, out_sem, to):
        return remote(
            raw.at[q, p], raw.at[q, p], out_sem.at[p, q], got.at[p, q], {"group": to}
        )

    def arrived(p, q):
        relay(p, q, up, g).wait_recv()

    def relay_up(p, q):
        @pl.when(g < planes - 1)
        def _():
            relay(p, q, up, g + 1).start()

    def relay_down(p, q):
        @pl.when(g > 0)
        def _():
            relay(p, q, down, g - 1).start()

    def other(i):
        return partner(c, jnp.where(i == 1, seqs - 1, i - 1), seqs)

    @pl.loop(1, seqs)
    def _(i):
        s = other(i)

        @pl.when(g < planes - 1)
        def _():
            own_out(s, 0, own_up, g + 1).start()

        @pl.when(g > 0)
        def _():
            own_out(s, 1, own_down, g - 1).start()

        @pl.when(i == 1)
        def _():
            @pl.when(g < planes - 1)
            def _():
                own_along(own_up, g + 1).start()

            @pl.when(g > 0)
            def _():
                own_along(own_down, g - 1).start()

    @pl.loop(1, seqs)
    def _(i):
        own_side(partner(c, i, seqs)).start()

    raw[c, g] = stage[c]
    loads[1].wait()
    wide[...] = key_stage[...].astype(jnp.float32)
    for h in range(heads):
        key_w[h * key_part : (h + 1) * key_part, :] = (
            wide[pl.ds(h, latent, stride=heads), :].T.astype(jnp.bfloat16)
        )

    loads[2].wait()
    loads[3].wait()
    wide[...] = value_stage[...].astype(jnp.float32)
    for h in range(heads):
        value_w[:, h * size : (h + 1) * size] = (
            wide[pl.ds(h, latent, stride=heads), :].astype(jnp.bfloat16)
        )

    low = 2 * g < planes

    def near_first(from_below, from_above):
        pl.when(low)(from_above)
        from_below()
        pl.when(jnp.logical_not(low))(from_above)

    @pl.loop(1, seqs)
    def _(i):
        s = other(i)

        def spread_below():
            @pl.when(g > 0)
            def _():
                own_out(s, 0, own_up, g).wait_recv()
                scatter(0, s, g - 1).start()

        def spread_above():
            @pl.when(g < planes - 1)
            def _():
                own_out(s, 1, own_down, g).wait_recv()
                scatter(1, s, g + 1).start()

        near_first(spread_below, spread_above)

        def own_below():
            @pl.when(g > 0)
            def _():
                arrived(g - 1, c)
                relay_up(g - 1, c)

        def own_above():
            @pl.when(g < planes - 1)
            def _():
                arrived(g + 1, c)
                relay_down(g + 1, c)

        @pl.when(i == 1)
        def _():
            near_first(own_below, own_above)

    def expand(q, u):
        first = u * per_unit
        x = jnp.concatenate(
            [
                raw[q, pl.ds(first, per_unit), k * blk : (k + 1) * blk, :]
                .astype(jnp.float32)
                .reshape(LANES, LANES)
                for k in range(slabs)
            ],
            axis=1,
        )
        mean = jnp.mean(x * x, axis=-1, keepdims=True)
        rows = (x * lax.rsqrt(mean + 1e-06) * gain[...]).astype(jnp.bfloat16)
        start = pl.multiple_of((q * planes + first) * blk, LANES)
        wide_keys = lax.dot_general(
            key_w[...], rows, (((1,), (1,)), ((), ())), preferred_element_type=jnp.float32
        ).astype(jnp.bfloat16)
        pieces = []
        for j in range(per_unit):
            both = raw[q, first + j, tail:, :].astype(jnp.float32)
            pieces += [both[:, :rotary], pltpu.roll(both, rotary, 1)[:, :rotary]]
        turned = jnp.concatenate(pieces, axis=0).T.astype(jnp.bfloat16)
        for h in range(heads):
            keys[h, :key_part, pl.ds(start, LANES)] = wide_keys[h * key_part : (h + 1) * key_part]
            keys[h, key_part:, pl.ds(start, LANES)] = turned
        wide_values = jnp.dot(rows, value_w[...], preferred_element_type=jnp.float32)
        for h in range(heads):
            mixed[pl.ds(h, LANES, stride=heads), :] = wide_values[:, h * size : (h + 1) * size]
        at = pl.multiple_of(start * heads, LANES * heads)
        values[pl.ds(at, LANES * heads), :] = mixed[...].astype(jnp.bfloat16)

    def settle(q, low, high):
        @pl.loop(0, planes // per_unit)
        def _(u):
            far = jnp.maximum(g - u * per_unit, (u + 1) * per_unit - 1 - g)
            far = jnp.maximum(far, 1)

            @pl.when((far >= low) & (far <= high))
            def _():
                expand(q, u)

    @pl.loop(1, seqs)
    def _(i):
        q = other(i)

        def next_below():
            @pl.when(g > 0)
            def _():
                arrived(g - 1, q)
                relay_up(g - 1, q)

        def next_above():
            @pl.when(g < planes - 1)
            def _():
                arrived(g + 1, q)
                relay_down(g + 1, q)

        near_first(next_below, next_above)

    @pl.loop(1, seqs)
    def _(i):
        arrived(g, other(i))

    @pl.loop(1, max(planes - 1, 2))
    def _(r):
        @pl.loop(0, seqs)
        def _(i):
            q = jnp.where(i == 0, c, other(i))
            below, above = g - 1 - r, g + 1 + r

            @pl.when(below >= 0)
            def _():
                arrived(below, q)
                relay_up(below, q)

            @pl.when(above < planes)
            def _():
                arrived(above, q)
                relay_down(above, q)

            settle(q, r, jnp.where(r == planes - 2, r + 1, r))

    @pl.loop(0, seqs)
    def _(s):
        @pl.when(g < planes - 1)
        def _():
            own_out(s, 0, own_up, g).wait_send()

        @pl.when(g > 0)
        def _():
            own_out(s, 1, own_down, g).wait_send()

        @pl.when(s != c)
        def _():
            own_side(s).wait_send()

            @pl.when(g > 0)
            def _():
                scatter(0, s, g).wait_send()

            @pl.when(g < planes - 1)
            def _():
                scatter(1, s, g).wait_send()

        @pl.loop(0, planes)
        def _(p):
            @pl.when((p < g) & (g < planes - 1))
            def _():
                relay(p, s, up, g).wait_send()

            @pl.when((p > g) & (g > 0))
            def _():
                relay(p, s, down, g).wait_send()


def store(keys, values, keys_out, values_out, sems):
    pieces = sems.shape[0] // 2
    rows = values.shape[0] // pieces
    heads = keys.shape[0] // pieces
    copies = []
    for i in range(pieces):
        part = pl.ds(i * heads, heads)
        copies.append(pltpu.make_async_copy(keys.at[part], keys_out.at[part], sems.at[2 * i]))
        part = pl.ds(i * rows, rows)
        copies.append(
            pltpu.make_async_copy(values.at[part], values_out.at[part], sems.at[2 * i + 1])
        )
    for copy in copies:
        copy.start()
    for copy in copies:
        copy.wait()


def per_device(latents, rotary_rows, latent_gain, key_up, value_up):
    seqs, planes = lax.axis_size("ctx"), lax.axis_size("group")
    _, blk, latent = latents.shape
    rotary = rotary_rows.shape[2]
    heads, key_part = key_up.shape[1:]
    size = value_up.shape[2]
    length = seqs * planes * blk
    packed = (blk * (latent + rotary) // LANES, LANES)
    bf16 = jnp.bfloat16
    dma = pltpu.SemaphoreType.DMA
    in_hbm = functools.partial(pltpu.with_memory_space_constraint, memory_space=pltpu.HBM)
    outer = pl.BlockSpec(memory_space=pltpu.HBM)
    inside = pl.BlockSpec(memory_space=pltpu.VMEM)
    keys, values = pl.pallas_call(
        functools.partial(kernel, seqs, planes, heads, rotary),
        out_shape=(
            pltpu.VMEM((heads, key_part + rotary, length), bf16),
            pltpu.VMEM((length * heads, size), bf16),
        ),
        in_specs=[outer] * 5,
        out_specs=(inside, inside),
        scratch_shapes=[
            pltpu.VMEM((seqs, *packed), bf16),
            pltpu.VMEM((seqs, planes, *packed), bf16),
            pltpu.VMEM((2, seqs, *packed), bf16),
            pltpu.VMEM((seqs, blk, rotary), bf16),
            pltpu.VMEM((latent * heads, key_part), bf16),
            pltpu.VMEM((latent * heads, size), bf16),
            pltpu.VMEM((latent * heads, size), jnp.float32),
            pltpu.VMEM((heads * key_part, latent), bf16),
            pltpu.VMEM((latent, heads * size), bf16),
            pltpu.VMEM((LANES * heads, size), jnp.float32),
            pltpu.VMEM((1, latent), jnp.float32),
            dma((latent // LANES,)),
            dma((4,)),
            dma((planes, seqs)),
            dma((2, seqs)),
            dma((seqs,)), dma((seqs,)), dma((seqs,)),
            dma((2, seqs)),
            dma((planes, seqs)), dma((planes, seqs)),
        ],
        compiler_params=pltpu.CompilerParams(
            collective_id=0, has_side_effects=True, vmem_limit_bytes=32 * 1024 * 1024
        ),
    )(
        in_hbm(latents),
        in_hbm(rotary_rows),
        in_hbm(latent_gain.reshape(1, latent)),
        in_hbm(key_up.reshape(latent * heads, key_part)),
        in_hbm(value_up.reshape(latent * heads, size)),
    )
    keys, values = pl.pallas_call(
        store,
        out_shape=(
            jax.ShapeDtypeStruct(keys.shape, bf16),
            jax.ShapeDtypeStruct(values.shape, bf16),
        ),
        in_specs=[inside, inside],
        out_specs=(outer, outer),
        scratch_shapes=[dma((2 * heads,))],
        compiler_params=pltpu.CompilerParams(vmem_limit_bytes=16 * 1024 * 1024),
    )(keys, values)
    return keys[None], values.reshape(1, length, heads, size)


def solution(mesh):
    in_specs = (
        P("ens", ("ctx", "group"), None),
        P("ens", ("ctx", "group"), None),
        P(),
        P("ens", "group", None),
        P("ens", "group", None),
    )
    out_specs = (P(("ens", "ctx"), "group", None, None), P(("ens", "ctx"), None, "group", None))
    return jax.shard_map(
        per_device, mesh=mesh, in_specs=in_specs, out_specs=out_specs, check_vma=False
    )
```

profile of v0, /device:TPU:0, one launch (start us, length us, event | category | flops | bytes accessed | tf_op | source)
XLA Modules:
  0.0 29.4 jit_solution(12788584473197460981)
XLA Ops:
  0.6 27.3 %shard_map.68 = (bf16[4,192,1024]{2,1,0:T(8,128)(2,1)S(1)}, bf16[4096,128]{1,0:T(8,128)(2,1)S(1)}) custom-call(bf16[4,64,512]{2,1,0:T(8,128)(2,1)} %lat.1, bf16[4,64,64]{2,1,0:T(8,128)(2,1)} %rot.1, f32[1,512]{1,0:T(1,128)} %bitcast.7, bf16[2048,128]{1,0:T(8,128)(2,1)} %bitcast.5, bf16[2048,128]{1,0:T(8,128)(2,1)} %bitcast.6), custom_call_target="tpu_custom_call" | custom-call | tf_op jit(solution)/shard_map/pallas_call | solution.py:359
  27.9 1.5 %shard_map.69 = (bf16[4,192,1024]{2,1,0:T(8,128)(2,1)}, bf16[4096,128]{1,0:T(8,128)(2,1)}) custom-call(bf16[4,192,1024]{2,1,0:T(8,128)(2,1)S(1)} %get-tuple-element.6.keys, bf16[4096,128]{1,0:T(8,128)(2,1)S(1)} %get-tuple-element.7.values), custom_call_target="tpu_custom_call" | custom-call | tf_op jit(solution)/shard_map/pallas_call | solution.py:397
where the time goes:
time: 29.6 us; the launch traced here: 29.4 us
  Pallas kernels  28.8 us (97%)
  between operations  0.64 us (2%)
    pallas_call x1, Pallas kernels, per_device(): pl.pallas_call(functools.partial(kernel, seqs, planes, heads, rotary), ou...  27.3 us
    pallas_call x1, Pallas kernels, per_device(): pl.pallas_call(store, out_shape=(jax.ShapeDtypeStruct(keys.shape, bf16),...  1.55 us

commit v1 on v0

v1 whole, which is shorter than its diff:
```python
import functools

import jax
import jax.numpy as jnp
from jax import lax
from jax.experimental import pallas as pl
from jax.experimental.pallas import tpu as pltpu
from jax.sharding import PartitionSpec as P

MESH = pl.DeviceIdType.MESH
LANES = 128
BF16 = jnp.bfloat16


def xor(me, step, count):
    total, bit = 0, 1
    while bit < count:
        total = total + bit * lax.rem(me // bit + step // bit, 2)
        bit *= 2
    return total


def partner(me, step, count):
    return lax.rem(me + step, count) if count & (count - 1) else xor(me, step, count)


def source(me, step, count):
    return lax.rem(me + count - step, count) if count & (count - 1) else xor(me, step, count)


def turn(i, count):
    return jnp.where(i == 1, count - 1, i - 1)


def pending(c, g, seqs, planes, units):
    q = source(c, turn(jnp.int32(seqs - 1), seqs), seqs) if seqs > 1 else c
    return q, jnp.where(2 * g < planes, units - 1, 0)


def expand(block, slabs, blk, per_unit, heads, rotary, gain, key_w, value_w, mixed, put_keys, put_values):
    key_part = key_w.shape[0] // heads
    size = value_w.shape[1] // heads
    x = jnp.concatenate(
        [block(k * blk, blk).astype(jnp.float32).reshape(LANES, LANES) for k in range(slabs)],
        axis=1,
    )
    mean = jnp.mean(x * x, axis=-1, keepdims=True)
    rows = (x * lax.rsqrt(mean + 1e-06) * gain[...]).astype(BF16)
    wide_keys = lax.dot_general(
        key_w[...], rows, (((1,), (1,)), ((), ())), preferred_element_type=jnp.float32
    ).astype(BF16)
    tails = block(slabs * blk, blk * rotary // LANES).astype(jnp.float32)
    pieces = []
    for j in range(per_unit):
        pieces += [tails[j][:, :rotary], pltpu.roll(tails[j], rotary, 1)[:, :rotary]]
    turned = jnp.concatenate(pieces, axis=0).T.astype(BF16)
    for h in range(heads):
        put_keys(h, wide_keys[h * key_part : (h + 1) * key_part], turned)
    wide_values = jnp.dot(rows, value_w[...], preferred_element_type=jnp.float32)
    for h in range(heads):
        mixed[pl.ds(h, LANES, stride=heads), :] = wide_values[:, h * size : (h + 1) * size]
    put_values(mixed[...].astype(BF16))


def kernel(
    seqs, planes, heads, rotary,
    lat, rot, gain_in, key_up, value_up,
    keys, values, last, key_w, value_w, gain,
    stage, raw, mid, rot_stage, key_stage, value_stage, wide, mixed,
    load_sem, got, mid_got, sent, ready,
):
    c, g = lax.axis_index("ctx"), lax.axis_index("group")
    blk, latent = lat.shape[1:]
    slabs = latent // LANES
    tail = slabs * blk
    half = blk // 2
    per_unit = LANES // blk
    units = planes // per_unit
    key_part = key_w.shape[0] // heads
    size = value_w.shape[1] // heads
    first = partner(c, seqs - 1, seqs)

    def lat_load(s, k, sem):
        return pltpu.make_async_copy(
            lat.at[s, :, pl.ds(k * LANES, LANES)],
            stage.at[s, pl.ds(k * blk, blk), :],
            load_sem.at[sem],
        )

    rot_load = pltpu.make_async_copy(rot, rot_stage, load_sem.at[0])
    for k in range(slabs):
        lat_load(first, k, 1).start()
    rot_load.start()

    @pl.loop(1, seqs)
    def _(b):
        for k in range(slabs):
            lat_load(partner(first, b, seqs), k, 2).start()

    loads = [
        pltpu.make_async_copy(key_up, key_stage, load_sem.at[3]),
        pltpu.make_async_copy(value_up, value_stage, load_sem.at[4]),
        pltpu.make_async_copy(gain_in, gain, load_sem.at[4]),
    ]
    for load in loads:
        load.start()

    barrier = pltpu.get_barrier_semaphore()
    above, below = g < planes - 1, g > 0

    @pl.when(above)
    def _():
        pl.semaphore_signal(barrier, inc=1, device_id={"group": g + 1}, device_id_type=MESH)

    @pl.loop(c + 1, seqs)
    def _(s):
        pl.semaphore_signal(barrier, inc=1, device_id={"ctx": s}, device_id_type=MESH)

    def remote(src, dst, in_sem, to):
        return pltpu.make_async_remote_copy(
            src_ref=src, dst_ref=dst, send_sem=sent, recv_sem=in_sem,
            device_id=to, device_id_type=MESH,
        )

    def out(way, i, s, part, to):
        return remote(
            stage.at[s, part], mid.at[way, 0, i - 1, part], mid_got.at[way, 0, i - 1], {"group": to}
        )

    def own_along(to):
        return remote(stage.at[c], raw.at[c, g], got.at[g, c], {"group": to})

    def own_side(s):
        return remote(stage.at[s], raw.at[c, g], got.at[g, c], {"ctx": s})

    def forward(way, i, to):
        return remote(mid.at[way, 0, i - 1], mid.at[way, 1, i - 1], mid_got.at[way, 1, i - 1], {"group": to})

    def scatter(way, far, i, p, s):
        return remote(mid.at[way, far, i - 1], raw.at[c, p], got.at[p, c], {"ctx": s})

    def relay(p, q, to):
        return remote(raw.at[q, p], raw.at[q, p], got.at[p, q], {"group": to})

    whole = pl.ds(0, stage.shape[1])
    wide_part, rot_part = pl.ds(0, tail), pl.ds(tail, half)

    def rest(way, to):
        @pl.loop(2, seqs)
        def _(i):
            out(way, i, partner(c, turn(i, seqs), seqs), whole, to).start()

    @pl.when(c + g > 0)
    def _():
        pl.semaphore_wait(barrier, c + jnp.minimum(g, 1))

    @pl.when(below)
    def _():
        pl.semaphore_signal(ready.at[0], inc=1, device_id={"group": g - 1}, device_id_type=MESH)

    @pl.loop(0, c)
    def _(s):
        pl.semaphore_signal(ready.at[1], inc=1, device_id={"ctx": s}, device_id_type=MESH)

    for k in range(slabs):
        lat_load(first, k, 1).wait()

    @pl.when(below)
    def _():
        out(1, 1, first, wide_part, g - 1).start()

    rot_load.wait()

    @pl.loop(0, seqs)
    def _(s):
        block = rot_stage[s].astype(jnp.float32)
        both = jnp.concatenate([block[:half], block[half:]], axis=1)
        stage[s, pl.ds(tail, half), :] = both.astype(BF16)

    @pl.loop(1, seqs)
    def _(b):
        for k in range(slabs):
            lat_load(partner(first, b, seqs), k, 2).wait()

    @pl.when(below)
    def _():
        out(1, 1, first, rot_part, g - 1).start()
        own_along(g - 1).start()
        rest(1, g - 1)

    @pl.when(above)
    def _():
        pl.semaphore_wait(ready.at[0], 1)
        out(0, 1, first, whole, g + 1).start()
        own_along(g + 1).start()
        rest(0, g + 1)

    @pl.when(c < seqs - 1)
    def _():
        pl.semaphore_wait(ready.at[1], seqs - 1 - c)

    @pl.loop(1, seqs)
    def _(i):
        own_side(partner(c, turn(i, seqs), seqs)).start()

    raw[c, g] = stage[c]
    loads[0].wait()
    wide[...] = key_stage[...].astype(jnp.float32)
    for h in range(heads):
        key_w[h * key_part : (h + 1) * key_part, :] = (
            wide[pl.ds(h, latent, stride=heads), :].T.astype(BF16)
        )
    loads[1].wait()
    loads[2].wait()
    wide[...] = value_stage[...].astype(jnp.float32)
    for h in range(heads):
        value_w[:, h * size : (h + 1) * size] = (
            wide[pl.ds(h, latent, stride=heads), :].astype(BF16)
        )

    low = 2 * g < planes

    def near_first(go):
        pl.when(low)(lambda: go(1))
        go(0)
        pl.when(jnp.logical_not(low))(lambda: go(1))

    def arrived(p, q):
        relay(p, q, g).wait_recv()

    def plane(way, far):
        return g - far if way == 0 else g + far

    def exists(way, far):
        return g >= far if way == 0 else g + far < planes

    def onward(way):
        return above if way == 0 else below

    def towards(way):
        return g + 1 if way == 0 else g - 1

    def along(far):
        def go(way):
            @pl.when(exists(way, far))
            def _():
                arrived(plane(way, far), c)

                @pl.when(onward(way))
                def _():
                    relay(plane(way, far), c, towards(way)).start()

        near_first(go)

    def inner(way, far):
        return g > far if way == 0 else g + far < planes - 1

    def pass_mid(far, i):
        def go(way):
            @pl.when(exists(way, far) if far == 1 else inner(way, far))
            def _():
                forward(way, i, g).wait_recv() if far == 2 else out(way, i, c, whole, g).wait_recv()
                s = partner(c, turn(i, seqs), seqs)
                scatter(way, far - 1, i, plane(way, far), s).start()
                if far == 1:
                    @pl.when(onward(way) & inner(way, 1))
                    def _():
                        forward(way, i, towards(way)).start()

        near_first(go)

    def take(far, i):
        def go(way):
            @pl.when(exists(way, far))
            def _():
                q = source(c, turn(i, seqs), seqs)
                arrived(plane(way, far), q)

                @pl.when(onward(way) & ((far > 1) | jnp.logical_not(inner(way, 1))))
                def _():
                    relay(plane(way, far), q, towards(way)).start()

        near_first(go)

    end_q, end_u = pending(c, g, seqs, planes, units)

    def settle(q, low_far, high_far):
        @pl.loop(0, units)
        def _(u):
            far = jnp.maximum(g - u * per_unit, (u + 1) * per_unit - 1 - g)
            far = jnp.maximum(far, 1)
            wanted = (far >= low_far) & (far <= high_far)

            @pl.when(wanted & ((q != end_q) | (u != end_u)))
            def _():
                begin = u * per_unit
                start = pl.multiple_of((q * planes + begin) * blk, LANES)

                def block(row, count):
                    return raw[q, pl.ds(begin, per_unit), row : row + count, :]

                def put_keys(h, wide_keys, turned):
                    keys[h, :key_part, pl.ds(start, LANES)] = wide_keys
                    keys[h, key_part:, pl.ds(start, LANES)] = turned

                def put_values(rows):
                    at = pl.multiple_of(start * heads, LANES * heads)
                    values[pl.ds(at, LANES * heads), :] = rows

                expand(
                    block, slabs, blk, per_unit, heads, rotary, gain, key_w, value_w, mixed,
                    put_keys, put_values,
                )

    @pl.loop(1, seqs)
    def _(i):
        pass_mid(1, i)

        @pl.when(i == 1)
        def _():
            along(1)

    @pl.loop(0, seqs)
    def _(i):
        @pl.when(i == 0)
        def _():
            along(2)

        @pl.when(i > 0)
        def _():
            pass_mid(2, i)
            q = source(c, turn(i, seqs), seqs)
            arrived(g, q)
            take(1, i)

        settle(jnp.where(i == 0, c, source(c, turn(i, seqs), seqs)), 1, 1)

    @pl.loop(2, max(planes, 3))
    def _(far):
        @pl.loop(0, seqs)
        def _(i):
            @pl.when((i == 0) & (far > 2))
            def _():
                along(far)

            @pl.when(i > 0)
            def _():
                take(far, i)

            settle(jnp.where(i == 0, c, source(c, turn(i, seqs), seqs)), far, far)

    last[...] = raw[end_q, pl.ds(end_u * per_unit, per_unit)]

    ups, downs = jnp.minimum(planes - 1 - g, 1), jnp.minimum(g, 1)
    total = seqs * (ups + downs) + (seqs - 1) * (1 + ups + downs)
    total = total + seqs * (g * ups + (planes - 1 - g) * downs)
    for far in (g, planes - 1 - g):
        total = total + (seqs - 1) * jnp.where(far > 2, 1, 0)

    @pl.loop(0, total)
    def _(_):
        own_along(g).wait_send()


def store(
    seqs, planes, heads, rotary, blk,
    keys, values, last, key_w, value_w, gain,
    keys_out, values_out,
    end_keys, end_values, mixed, sems,
):
    c, g = lax.axis_index("ctx"), lax.axis_index("group")
    slabs = gain.shape[1] // LANES
    per_unit = LANES // blk
    units = planes // per_unit
    key_part = key_w.shape[0] // heads
    blocks = seqs * units
    end_q, end_u = pending(c, g, seqs, planes, units)
    end = end_q * units + end_u

    def columns(b):
        return pl.ds(pl.multiple_of(b * LANES, LANES), LANES)

    def rows(b):
        return pl.ds(pl.multiple_of(b * LANES * heads, LANES * heads), LANES * heads)

    @pl.loop(1, blocks)
    def _(j):
        b = lax.rem(end + j, blocks)
        pltpu.make_async_copy(
            keys.at[:, :, columns(b)], keys_out.at[:, :, columns(b)], sems.at[0]
        ).start()
        pltpu.make_async_copy(values.at[rows(b)], values_out.at[rows(b)], sems.at[1]).start()

    def block(row, count):
        return last[:, row : row + count, :]

    def put_keys(h, wide_keys, turned):
        end_keys[h, :key_part, :] = wide_keys
        end_keys[h, key_part:, :] = turned

    def put_values(part):
        end_values[...] = part

    expand(
        block, slabs, blk, per_unit, heads, rotary, gain, key_w, value_w, mixed,
        put_keys, put_values,
    )
    pltpu.make_async_copy(end_keys, keys_out.at[:, :, columns(end)], sems.at[0]).start()
    pltpu.make_async_copy(end_values, values_out.at[rows(end)], sems.at[1]).start()
    pltpu.make_async_copy(keys, keys_out, sems.at[0]).wait()
    pltpu.make_async_copy(values, values_out, sems.at[1]).wait()


def per_device(latents, rotary_rows, latent_gain, key_up, value_up):
    seqs, planes = lax.axis_size("ctx"), lax.axis_size("group")
    _, blk, latent = latents.shape
    rotary = rotary_rows.shape[2]
    heads, key_part = key_up.shape[1:]
    size = value_up.shape[2]
    length = seqs * planes * blk
    per_unit = LANES // blk
    packed = (blk * (latent + rotary) // LANES, LANES)
    dma = pltpu.SemaphoreType.DMA
    in_hbm = functools.partial(pltpu.with_memory_space_constraint, memory_space=pltpu.HBM)
    outer = pl.BlockSpec(memory_space=pltpu.HBM)
    inside = pl.BlockSpec(memory_space=pltpu.VMEM)
    held = pl.pallas_call(
        functools.partial(kernel, seqs, planes, heads, rotary),
        out_shape=(
            pltpu.VMEM((heads, key_part + rotary, length), BF16),
            pltpu.VMEM((length * heads, size), BF16),
            pltpu.VMEM((per_unit, *packed), BF16),
            pltpu.VMEM((heads * key_part, latent), BF16),
            pltpu.VMEM((latent, heads * size), BF16),
            pltpu.VMEM((1, latent), jnp.float32),
        ),
        in_specs=[outer] * 5,
        out_specs=(inside,) * 6,
        scratch_shapes=[
            pltpu.VMEM((seqs, *packed), BF16),
            pltpu.VMEM((seqs, planes, *packed), BF16),
            pltpu.VMEM((2, 2, seqs - 1, *packed), BF16),
            pltpu.VMEM((seqs, blk, rotary), BF16),
            pltpu.VMEM((latent * heads, key_part), BF16),
            pltpu.VMEM((latent * heads, size), BF16),
            pltpu.VMEM((latent * heads, size), jnp.float32),
            pltpu.VMEM((LANES * heads, size), jnp.float32),
            dma((5,)),
            dma((planes, seqs)),
            dma((2, 2, seqs - 1)),
            dma,
            pltpu.SemaphoreType.REGULAR((2,)),
        ],
        compiler_params=pltpu.CompilerParams(
            collective_id=0, has_side_effects=True, vmem_limit_bytes=32 * 1024 * 1024
        ),
    )(
        in_hbm(latents),
        in_hbm(rotary_rows),
        in_hbm(latent_gain.reshape(1, latent)),
        in_hbm(key_up.reshape(latent * heads, key_part)),
        in_hbm(value_up.reshape(latent * heads, size)),
    )
    keys, values = pl.pallas_call(
        functools.partial(store, seqs, planes, heads, rotary, blk),
        out_shape=(
            jax.ShapeDtypeStruct((heads, key_part + rotary, length), BF16),
            jax.ShapeDtypeStruct((length * heads, size), BF16),
        ),
        in_specs=[inside] * 6,
        out_specs=(outer, outer),
        scratch_shapes=[
            pltpu.VMEM((heads, key_part + rotary, LANES), BF16),
            pltpu.VMEM((LANES * heads, size), BF16),
            pltpu.VMEM((LANES * heads, size), jnp.float32),
            dma((2,)),
        ],
        compiler_params=pltpu.CompilerParams(vmem_limit_bytes=16 * 1024 * 1024),
    )(*held)
    return keys[None], values.reshape(1, length, heads, size)


def solution(mesh):
    in_specs = (
        P("ens", ("ctx", "group"), None),
        P("ens", ("ctx", "group"), None),
        P(),
        P("ens", "group", None),
        P("ens", "group", None),
    )
    out_specs = (P(("ens", "ctx"), "group", None, None), P(("ens", "ctx"), None, "group", None))
    return jax.shard_map(
        per_device, mesh=mesh, in_specs=in_specs, out_specs=out_specs, check_vma=False
    )
```

time: 29.6 us -> 27.7 us (0.936)
  Pallas kernels: 28.8 us -> 26.9 us
    pallas_call x1, Pallas kernels: 27.3 us -> 25.4 us  [per_device(): pl.pallas_call(functools.partial(kernel, seqs, planes, heads, rotary), ou...]
where the time goes in v1:
time: 27.7 us; the launch traced here: 27.6 us
  Pallas kernels  26.9 us (97%)
  between operations  0.64 us (2%)
    pallas_call x1, Pallas kernels, per_device(): pl.pallas_call(functools.partial(kernel, seqs, planes, heads, rotary), ou...  25.4 us
    pallas_call x1, Pallas kernels, per_device(): pl.pallas_call(functools.partial(store, seqs, planes, heads, rotary, blk)...  1.51 us

profile of v1, /device:TPU:0, one launch (start us, length us, event | category | flops | bytes accessed | tf_op | source)
XLA Modules:
  0.0 27.6 jit_solution(13799726350642153035)
XLA Ops:
  0.6 25.4 %shard_map.68 = (bf16[4,192,1024]{2,1,0:T(8,128)(2,1)S(1)}, bf16[4096,128]{1,0:T(8,128)(2,1)S(1)}, bf16[2,288,128]{2,1,0:T(8,128)(2,1)S(1)}, bf16[512,512]{1,0:T...) custom-call(bf16[4,64,512]{2,1,0:T(8,128)(2,1)} %lat.1, bf16[4,64,64]{2,1,0:T(8,128)(2,1)} %rot.1, ...), custom_call_target="tpu_custom_call" | custom-call | tf_op jit(solution)/shard_map/pallas_call | solution.py:427
  26.1 1.5 %shard_map.69 = (bf16[4,192,1024]{2,1,0:T(8,128)(2,1)}, bf16[4096,128]{1,0:T(8,128)(2,1)}) custom-call(bf16[4,192,1024]{2,1,0:T(8,128)(2,1)S(1)} %get-tuple-element.10.keys, bf16[4096,128]{1,0:T(8,128)(2,1)S(1)} %get-tuple-element.11.values, bf16[2,288,128]{2,1,0:T(8,128)(2,1)S(1)} %get-tuple-element.12.last, bf16[512,512]{1,0:T(8,128)(2,1)S(1)} %get-tuple-element.13.key_w, ...), custom_call_target="tpu_custom_call" | custom-call | tf_op jit(solution)/shard_map/pallas_call | solution.py:464

commit v2 on v1

--- a/solution.py
+++ b/solution.py
@@ -10,6 +10,7 @@
 MESH = pl.DeviceIdType.MESH
 LANES = 128
 BF16 = jnp.bfloat16
+SHIFT, DELAY = False, False
 
 
 def xor(me, step, count):
@@ -69,7 +70,7 @@
     stage, raw, mid, rot_stage, key_stage, value_stage, wide, mixed,
     load_sem, got, mid_got, sent, ready,
 ):
-    c, g = lax.axis_index("ctx"), lax.axis_index("group")
+    ens, c, g = lax.axis_index("ens"), lax.axis_index("ctx"), lax.axis_index("group")
     blk, latent = lat.shape[1:]
     slabs = latent // LANES
     tail = slabs * blk
@@ -107,6 +108,10 @@
 
     barrier = pltpu.get_barrier_semaphore()
     above, below = g < planes - 1, g > 0
+    edge = (g == 0) | (g == planes - 1)
+
+    def inner(way, far):
+        return g > far if way == 0 else g + far < planes - 1
 
     @pl.when(above)
     def _():
@@ -162,10 +167,28 @@
     def _(s):
         pl.semaphore_signal(ready.at[1], inc=1, device_id={"ctx": s}, device_id_type=MESH)
 
+    def prepare():
+        loads[0].wait()
+        wide[...] = key_stage[...].astype(jnp.float32)
+        for h in range(heads):
+            key_w[h * key_part : (h + 1) * key_part, :] = (
+                wide[pl.ds(h, latent, stride=heads), :].T.astype(BF16)
+            )
+        loads[1].wait()
+        loads[2].wait()
+        wide[...] = value_stage[...].astype(jnp.float32)
+        for h in range(heads):
+            value_w[:, h * size : (h + 1) * size] = (
+                wide[pl.ds(h, latent, stride=heads), :].astype(BF16)
+            )
+
+    if DELAY:
+        pl.when(ens > 0)(prepare)
+
     for k in range(slabs):
         lat_load(first, k, 1).wait()
 
-    @pl.when(below)
+    @pl.when(below & above)
     def _():
         out(1, 1, first, wide_part, g - 1).start()
 
@@ -182,18 +205,24 @@
         for k in range(slabs):
             lat_load(partner(first, b, seqs), k, 2).wait()
 
-    @pl.when(below)
+    @pl.when(below & above)
     def _():
         out(1, 1, first, rot_part, g - 1).start()
-        own_along(g - 1).start()
         rest(1, g - 1)
-
-    @pl.when(above)
-    def _():
+        pl.when(jnp.logical_not(inner(1, 1)))(lambda: own_along(g - 1).start())
         pl.semaphore_wait(ready.at[0], 1)
         out(0, 1, first, whole, g + 1).start()
+        rest(0, g + 1)
+        pl.when(jnp.logical_not(inner(0, 1)))(lambda: own_along(g + 1).start())
+
+    @pl.when(below & (g == planes - 1))
+    def _():
+        own_along(g - 1).start()
+
+    @pl.when(above & (g == 0))
+    def _():
+        pl.semaphore_wait(ready.at[0], 1)
         own_along(g + 1).start()
-        rest(0, g + 1)
 
     @pl.when(c < seqs - 1)
     def _():
@@ -204,19 +233,7 @@
         own_side(partner(c, turn(i, seqs), seqs)).start()
 
     raw[c, g] = stage[c]
-    loads[0].wait()
-    wide[...] = key_stage[...].astype(jnp.float32)
-    for h in range(heads):
-        key_w[h * key_part : (h + 1) * key_part, :] = (
-            wide[pl.ds(h, latent, stride=heads), :].T.astype(BF16)
-        )
-    loads[1].wait()
-    loads[2].wait()
-    wide[...] = value_stage[...].astype(jnp.float32)
-    for h in range(heads):
-        value_w[:, h * size : (h + 1) * size] = (
-            wide[pl.ds(h, latent, stride=heads), :].astype(BF16)
-        )
+    pl.when(ens == 0)(prepare) if DELAY else prepare()
 
     low = 2 * g < planes
 
@@ -252,18 +269,20 @@
 
         near_first(go)
 
-    def inner(way, far):
-        return g > far if way == 0 else g + far < planes - 1
+    def direct(way, far, origin, i):
+        if way == 0 or not SHIFT:
+            return inner(way, far)
+        return inner(way, far) & ((origin > 0) | (i > 1))
 
     def pass_mid(far, i):
         def go(way):
-            @pl.when(exists(way, far) if far == 1 else inner(way, far))
+            @pl.when(inner(way, far) if far == 1 else direct(way, far, c, i))
             def _():
                 forward(way, i, g).wait_recv() if far == 2 else out(way, i, c, whole, g).wait_recv()
                 s = partner(c, turn(i, seqs), seqs)
                 scatter(way, far - 1, i, plane(way, far), s).start()
                 if far == 1:
-                    @pl.when(onward(way) & inner(way, 1))
+                    @pl.when(onward(way) & direct(way, 1, c, i))
                     def _():
                         forward(way, i, towards(way)).start()
 
@@ -276,7 +295,7 @@
                 q = source(c, turn(i, seqs), seqs)
                 arrived(plane(way, far), q)
 
-                @pl.when(onward(way) & ((far > 1) | jnp.logical_not(inner(way, 1))))
+                @pl.when(onward(way) & ((far > 1) | jnp.logical_not(direct(way, 1, q, i))))
                 def _():
                     relay(plane(way, far), q, towards(way)).start()
 
@@ -312,28 +331,42 @@
                     put_keys, put_values,
                 )
 
+    def own(i):
+        q = source(c, turn(i, seqs), seqs)
+        arrived(g, q)
+
+        @pl.when(above & (g == 0))
+        def _():
+            relay(g, q, g + 1).start()
+
+        @pl.when(below & (g == planes - 1))
+        def _():
+            relay(g, q, g - 1).start()
+
     @pl.loop(1, seqs)
     def _(i):
         pass_mid(1, i)
-
-        @pl.when(i == 1)
-        def _():
-            along(1)
-
-    @pl.loop(0, seqs)
+        pl.when(edge)(lambda: own(i))
+
+    pl.when(inner(1, 1) & below)(lambda: own_along(g - 1).start())
+    pl.when(inner(0, 1) & above)(lambda: own_along(g + 1).start())
+    pl.when(jnp.logical_not(edge))(lambda: along(1))
+
+    @pl.loop(1, seqs + 1)
     def _(i):
-        @pl.when(i == 0)
-        def _():
-            along(2)
-
-        @pl.when(i > 0)
+        @pl.when(i < seqs)
         def _():
             pass_mid(2, i)
-            q = source(c, turn(i, seqs), seqs)
-            arrived(g, q)
+            pl.when(jnp.logical_not(edge))(lambda: own(i))
             take(1, i)
 
-        settle(jnp.where(i == 0, c, source(c, turn(i, seqs), seqs)), 1, 1)
+        @pl.when(i == seqs)
+        def _():
+            pl.when(edge)(lambda: along(1))
+
+        settle(jnp.where(i == seqs, c, source(c, turn(i, seqs), seqs)), 1, 1)
+
+    along(2)
 
     @pl.loop(2, max(planes, 3))
     def _(far):
@@ -352,10 +385,12 @@
     last[...] = raw[end_q, pl.ds(end_u * per_unit, per_unit)]
 
     ups, downs = jnp.minimum(planes - 1 - g, 1), jnp.minimum(g, 1)
-    total = seqs * (ups + downs) + (seqs - 1) * (1 + ups + downs)
-    total = total + seqs * (g * ups + (planes - 1 - g) * downs)
-    for far in (g, planes - 1 - g):
-        total = total + (seqs - 1) * jnp.where(far > 2, 1, 0)
+    total = seqs * (ups + downs + g * ups + (planes - 1 - g) * downs)
+    spread = sum(jnp.where(inner(way, far), 1, 0) for way in (0, 1) for far in (1, 2))
+    total = total + (seqs - 1) * (1 + spread)
+    if SHIFT:
+        here, there = jnp.where(c == 0, 1, 0), jnp.where(c == seqs - 1, 1, 0)
+        total = total + jnp.where(inner(1, 1) & below, there - here, 0) - jnp.where(inner(1, 2), here, 0)
 
     @pl.loop(0, total)
     def _(_):

time: 27.7 us -> 26.2 us (0.946)
  Pallas kernels: 26.9 us -> 25.4 us
    pallas_call x1, Pallas kernels: 25.4 us -> 23.9 us  [per_device(): pl.pallas_call(functools.partial(kernel, seqs, planes, heads, rotary), ou...]
where the time goes in v2:
time: 26.2 us; the launch traced here: 26.1 us
  Pallas kernels  25.4 us (97%)
  between operations  0.64 us (2%)
    pallas_call x1, Pallas kernels, per_device(): pl.pallas_call(functools.partial(kernel, seqs, planes, heads, rotary), ou...  23.9 us
    pallas_call x1, Pallas kernels, per_device(): pl.pallas_call(functools.partial(store, seqs, planes, heads, rotary, blk)...  1.51 us

profile of v2, /device:TPU:0, one launch (start us, length us, event | category | flops | bytes accessed | tf_op | source)
XLA Modules:
  0.0 26.1 jit_solution(13518370716221089751)
XLA Ops:
  0.6 23.9 %shard_map.68 = (bf16[4,192,1024]{2,1,0:T(8,128)(2,1)S(1)}, bf16[4096,128]{1,0:T(8,128)(2,1)S(1)}, bf16[2,288,128]{2,1,0:T(8,128)(2,1)S(1)}, bf16[512,512]{1,0:T...) custom-call(bf16[4,64,512]{2,1,0:T(8,128)(2,1)} %lat.1, bf16[4,64,64]{2,1,0:T(8,128)(2,1)} %rot.1, ...), custom_call_target="tpu_custom_call" | custom-call | tf_op jit(solution)/shard_map/pallas_call | solution.py:462
  24.5 1.5 %shard_map.69 = (bf16[4,192,1024]{2,1,0:T(8,128)(2,1)}, bf16[4096,128]{1,0:T(8,128)(2,1)}) custom-call(bf16[4,192,1024]{2,1,0:T(8,128)(2,1)S(1)} %get-tuple-element.10.keys, bf16[4096,128]{1,0:T(8,128)(2,1)S(1)} %get-tuple-element.11.values, bf16[2,288,128]{2,1,0:T(8,128)(2,1)S(1)} %get-tuple-element.12.last, bf16[512,512]{1,0:T(8,128)(2,1)S(1)} %get-tuple-element.13.key_w, ...), custom_call_target="tpu_custom_call" | custom-call | tf_op jit(solution)/shard_map/pallas_call | solution.py:499

commit v3 on v2

--- a/solution.py
+++ b/solution.py
@@ -10,7 +10,8 @@
 MESH = pl.DeviceIdType.MESH
 LANES = 128
 BF16 = jnp.bfloat16
-SHIFT, DELAY = False, False
+SHIFT = 1
+HELD = 0
 
 
 def xor(me, step, count):
@@ -29,12 +30,28 @@
     return lax.rem(me + count - step, count) if count & (count - 1) else xor(me, step, count)
 
 
-def turn(i, count):
-    return jnp.where(i == 1, count - 1, i - 1)
+def join(a, b, count):
+    if count & (count - 1):
+        return jnp.maximum(a, b)
+    total, bit = 0, 1
+    while bit < count:
+        total = total + bit * jnp.maximum(lax.rem(a // bit, 2), lax.rem(b // bit, 2))
+        bit *= 2
+    return total
+
+
+def lower(c, count):
+    if count & (count - 1):
+        return c
+    total, bit = 1, 1
+    while bit < count:
+        total = total * (1 + lax.rem(c // bit, 2))
+        bit *= 2
+    return total - 1
 
 
 def pending(c, g, seqs, planes, units):
-    q = source(c, turn(jnp.int32(seqs - 1), seqs), seqs) if seqs > 1 else c
+    q = source(c, seqs - 1, seqs) if seqs > 1 else c
     return q, jnp.where(2 * g < planes, units - 1, 0)
 
 
@@ -75,11 +92,12 @@
     slabs = latent // LANES
     tail = slabs * blk
     half = blk // 2
+    ways = mid.shape[0]
     per_unit = LANES // blk
     units = planes // per_unit
     key_part = key_w.shape[0] // heads
     size = value_w.shape[1] // heads
-    first = partner(c, seqs - 1, seqs)
+    first = partner(c, 1, seqs)
 
     def lat_load(s, k, sem):
         return pltpu.make_async_copy(
@@ -100,8 +118,8 @@
 
     loads = [
         pltpu.make_async_copy(key_up, key_stage, load_sem.at[3]),
-        pltpu.make_async_copy(value_up, value_stage, load_sem.at[4]),
-        pltpu.make_async_copy(gain_in, gain, load_sem.at[4]),
+        pltpu.make_async_copy(value_up, value_stage, load_sem.at[3]),
+        pltpu.make_async_copy(gain_in, gain, load_sem.at[3]),
     ]
     for load in loads:
         load.start()
@@ -109,6 +127,7 @@
     barrier = pltpu.get_barrier_semaphore()
     above, below = g < planes - 1, g > 0
     edge = (g == 0) | (g == planes - 1)
+    gate = (g == 1) | (g == planes - 2) if planes > 3 and HELD else g < 0
 
     def inner(way, far):
         return g > far if way == 0 else g + far < planes - 1
@@ -117,9 +136,15 @@
     def _():
         pl.semaphore_signal(barrier, inc=1, device_id={"group": g + 1}, device_id_type=MESH)
 
+    @pl.when(gate & (ens == 1))
+    def _():
+        pl.semaphore_signal(barrier, inc=1, device_id={"ens": 0}, device_id_type=MESH)
+
     @pl.loop(c + 1, seqs)
     def _(s):
-        pl.semaphore_signal(barrier, inc=1, device_id={"ctx": s}, device_id_type=MESH)
+        @pl.when(join(c, s, seqs) == s)
+        def _():
+            pl.semaphore_signal(barrier, inc=1, device_id={"ctx": s}, device_id_type=MESH)
 
     def remote(src, dst, in_sem, to):
         return pltpu.make_async_remote_copy(
@@ -129,7 +154,7 @@
 
     def out(way, i, s, part, to):
         return remote(
-            stage.at[s, part], mid.at[way, 0, i - 1, part], mid_got.at[way, 0, i - 1], {"group": to}
+            stage.at[s, part], mid.at[way % ways, 0, i - 1, part], mid_got.at[way % ways, 0, i - 1], {"group": to}
         )
 
     def own_along(to):
@@ -139,10 +164,10 @@
         return remote(stage.at[s], raw.at[c, g], got.at[g, c], {"ctx": s})
 
     def forward(way, i, to):
-        return remote(mid.at[way, 0, i - 1], mid.at[way, 1, i - 1], mid_got.at[way, 1, i - 1], {"group": to})
+        return remote(mid.at[way % ways, 0, i - 1], mid.at[way % ways, 1, i - 1], mid_got.at[way % ways, 1, i - 1], {"group": to})
 
     def scatter(way, far, i, p, s):
-        return remote(mid.at[way, far, i - 1], raw.at[c, p], got.at[p, c], {"ctx": s})
+        return remote(mid.at[way % ways, far, i - 1], raw.at[c, p], got.at[p, c], {"ctx": s})
 
     def relay(p, q, to):
         return remote(raw.at[q, p], raw.at[q, p], got.at[p, q], {"group": to})
@@ -153,11 +178,13 @@
     def rest(way, to):
         @pl.loop(2, seqs)
         def _(i):
-            out(way, i, partner(c, turn(i, seqs), seqs), whole, to).start()
-
-    @pl.when(c + g > 0)
-    def _():
-        pl.semaphore_wait(barrier, c + jnp.minimum(g, 1))
+            out(way, i, partner(c, i, seqs), whole, to).start()
+
+    early = lower(c, seqs) + jnp.minimum(g, 1) + jnp.where(gate & (ens == 0), 1, 0)
+
+    @pl.when(early > 0)
+    def _():
+        pl.semaphore_wait(barrier, early)
 
     @pl.when(below)
     def _():
@@ -165,25 +192,23 @@
 
     @pl.loop(0, c)
     def _(s):
-        pl.semaphore_signal(ready.at[1], inc=1, device_id={"ctx": s}, device_id_type=MESH)
+        @pl.when(join(c, s, seqs) == c)
+        def _():
+            pl.semaphore_signal(ready.at[2 + c], inc=1, device_id={"ctx": s}, device_id_type=MESH)
 
     def prepare():
-        loads[0].wait()
+        for load in loads:
+            load.wait()
         wide[...] = key_stage[...].astype(jnp.float32)
         for h in range(heads):
             key_w[h * key_part : (h + 1) * key_part, :] = (
                 wide[pl.ds(h, latent, stride=heads), :].T.astype(BF16)
             )
-        loads[1].wait()
-        loads[2].wait()
         wide[...] = value_stage[...].astype(jnp.float32)
         for h in range(heads):
             value_w[:, h * size : (h + 1) * size] = (
                 wide[pl.ds(h, latent, stride=heads), :].astype(BF16)
             )
-
-    if DELAY:
-        pl.when(ens > 0)(prepare)
 
     for k in range(slabs):
         lat_load(first, k, 1).wait()
@@ -224,16 +249,24 @@
         pl.semaphore_wait(ready.at[0], 1)
         own_along(g + 1).start()
 
-    @pl.when(c < seqs - 1)
-    def _():
-        pl.semaphore_wait(ready.at[1], seqs - 1 - c)
-
-    @pl.loop(1, seqs)
-    def _(i):
-        own_side(partner(c, turn(i, seqs), seqs)).start()
+    @pl.loop(c, seqs)
+    def _(t):
+        @pl.when(join(c, t, seqs) == t)
+        def _():
+            @pl.when(t > c)
+            def _():
+                pl.semaphore_wait(ready.at[2 + t], 1)
+
+            @pl.loop(1, seqs)
+            def _(i):
+                s = partner(c, i, seqs)
+
+                @pl.when(join(c, s, seqs) == t)
+                def _():
+                    own_side(s).start()
 
     raw[c, g] = stage[c]
-    pl.when(ens == 0)(prepare) if DELAY else prepare()
+    prepare()
 
     low = 2 * g < planes
 
@@ -272,14 +305,14 @@
     def direct(way, far, origin, i):
         if way == 0 or not SHIFT:
             return inner(way, far)
-        return inner(way, far) & ((origin > 0) | (i > 1))
+        return inner(way, far) & ((origin > 0) | (i != SHIFT) | (ens > 0))
 
     def pass_mid(far, i):
         def go(way):
             @pl.when(inner(way, far) if far == 1 else direct(way, far, c, i))
             def _():
                 forward(way, i, g).wait_recv() if far == 2 else out(way, i, c, whole, g).wait_recv()
-                s = partner(c, turn(i, seqs), seqs)
+                s = partner(c, i, seqs)
                 scatter(way, far - 1, i, plane(way, far), s).start()
                 if far == 1:
                     @pl.when(onward(way) & direct(way, 1, c, i))
@@ -288,11 +321,15 @@
 
         near_first(go)
 
-    def take(far, i):
+    def take(far, i, chain=None):
         def go(way):
-            @pl.when(exists(way, far))
-            def _():
-                q = source(c, turn(i, seqs), seqs)
+            wanted = exists(way, far)
+            if chain is not None:
+                wanted = wanted & (inner(way, far) != chain)
+
+            @pl.when(wanted)
+            def _():
+                q = source(c, i, seqs)
                 arrived(plane(way, far), q)
 
                 @pl.when(onward(way) & ((far > 1) | jnp.logical_not(direct(way, 1, q, i))))
@@ -332,7 +369,7 @@
                 )
 
     def own(i):
-        q = source(c, turn(i, seqs), seqs)
+        q = source(c, i, seqs)
         arrived(g, q)
 
         @pl.when(above & (g == 0))
@@ -345,26 +382,42 @@
 
     @pl.loop(1, seqs)
     def _(i):
-        pass_mid(1, i)
-        pl.when(edge)(lambda: own(i))
+        pl.when(g == planes - 1)(lambda: own(i))
+        pl.when((g < planes - 1) | (g == 0))(lambda: pass_mid(1, i))
+        pl.when((g == 0) & above)(lambda: own(i))
+
+    @pl.loop(1, seqs)
+    def _(i):
+        pl.when((g == planes - 1) & below)(lambda: pass_mid(1, i))
 
     pl.when(inner(1, 1) & below)(lambda: own_along(g - 1).start())
     pl.when(inner(0, 1) & above)(lambda: own_along(g + 1).start())
     pl.when(jnp.logical_not(edge))(lambda: along(1))
 
+    @pl.when(jnp.logical_not(edge))
+    def _():
+        settle(c, 1, 1)
+
+        @pl.loop(1, seqs)
+        def _(i):
+            take(1, i, True)
+
     @pl.loop(1, seqs + 1)
     def _(i):
         @pl.when(i < seqs)
         def _():
             pass_mid(2, i)
             pl.when(jnp.logical_not(edge))(lambda: own(i))
-            take(1, i)
-
-        @pl.when(i == seqs)
-        def _():
-            pl.when(edge)(lambda: along(1))
-
-        settle(jnp.where(i == seqs, c, source(c, turn(i, seqs), seqs)), 1, 1)
+            pl.when(edge)(lambda: take(1, i))
+            pl.when(jnp.logical_not(edge))(lambda: take(1, i, False))
+
+        @pl.when((i == seqs) & edge)
+        def _():
+            along(1)
+
+        @pl.when((i < seqs) | edge)
+        def _():
+            settle(jnp.where(i == seqs, c, source(c, i, seqs)), 1, 1)
 
     along(2)
 
@@ -376,11 +429,21 @@
             def _():
                 along(far)
 
+            turn = gate & (far == planes - 2)
+
+            @pl.when(turn & (ens == 1) & (i == max(seqs - HELD, 1)))
+            def _():
+                pl.semaphore_wait(ready.at[1], 1)
+
             @pl.when(i > 0)
             def _():
                 take(far, i)
 
-            settle(jnp.where(i == 0, c, source(c, turn(i, seqs), seqs)), far, far)
+            @pl.when(turn & (ens == 0) & (i == seqs - 1))
+            def _():
+                pl.semaphore_signal(ready.at[1], inc=1, device_id={"ens": 1}, device_id_type=MESH)
+
+            settle(jnp.where(i == 0, c, source(c, i, seqs)), far, far)
 
     last[...] = raw[end_q, pl.ds(end_u * per_unit, per_unit)]
 
@@ -389,8 +452,9 @@
     spread = sum(jnp.where(inner(way, far), 1, 0) for way in (0, 1) for far in (1, 2))
     total = total + (seqs - 1) * (1 + spread)
     if SHIFT:
-        here, there = jnp.where(c == 0, 1, 0), jnp.where(c == seqs - 1, 1, 0)
-        total = total + jnp.where(inner(1, 1) & below, there - here, 0) - jnp.where(inner(1, 2), here, 0)
+        here, there = jnp.where(c == 0, 1, 0), jnp.where(c == partner(0, SHIFT, seqs), 1, 0)
+        change = jnp.where(inner(1, 1) & below, there - here, 0) - jnp.where(inner(1, 2), here, 0)
+        total = total + jnp.where(ens == 0, change, 0)
 
     @pl.loop(0, total)
     def _(_):
@@ -454,6 +518,7 @@
     size = value_up.shape[2]
     length = seqs * planes * blk
     per_unit = LANES // blk
+    ways = 1 if planes <= 4 else 2
     packed = (blk * (latent + rotary) // LANES, LANES)
     dma = pltpu.SemaphoreType.DMA
     in_hbm = functools.partial(pltpu.with_memory_space_constraint, memory_space=pltpu.HBM)
@@ -474,17 +539,17 @@
         scratch_shapes=[
             pltpu.VMEM((seqs, *packed), BF16),
             pltpu.VMEM((seqs, planes, *packed), BF16),
-            pltpu.VMEM((2, 2, seqs - 1, *packed), BF16),
+            pltpu.VMEM((ways, 2, seqs - 1, *packed), BF16),
             pltpu.VMEM((seqs, blk, rotary), BF16),
             pltpu.VMEM((latent * heads, key_part), BF16),
             pltpu.VMEM((latent * heads, size), BF16),
             pltpu.VMEM((latent * heads, size), jnp.float32),
             pltpu.VMEM((LANES * heads, size), jnp.float32),
-            dma((5,)),
+            dma((4,)),
             dma((planes, seqs)),
-            dma((2, 2, seqs - 1)),
+            dma((ways, 2, seqs - 1)),
             dma,
-            pltpu.SemaphoreType.REGULAR((2,)),
+            pltpu.SemaphoreType.REGULAR((2 + seqs,)),
         ],
         compiler_params=pltpu.CompilerParams(
             collective_id=0, has_side_effects=True, vmem_limit_bytes=32 * 1024 * 1024

time: 26.2 us -> 25.5 us (0.973)
  Pallas kernels: 25.4 us -> 24.7 us
    pallas_call x1, Pallas kernels: 23.9 us -> 23.2 us  [per_device(): pl.pallas_call(functools.partial(kernel, seqs, planes, heads, rotary), ou...]
where the time goes in v3:
time: 25.5 us; the launch traced here: 25.3 us
  Pallas kernels  24.7 us (97%)
  between operations  0.64 us (3%)
    pallas_call x1, Pallas kernels, per_device(): pl.pallas_call(functools.partial(kernel, seqs, planes, heads, rotary), ou...  23.2 us
    pallas_call x1, Pallas kernels, per_device(): pl.pallas_call(functools.partial(store, seqs, planes, heads, rotary, blk)...  1.51 us

profile of v3, /device:TPU:0, one launch (start us, length us, event | category | flops | bytes accessed | tf_op | source)
XLA Modules:
  0.0 25.3 jit_solution(12909721653707718336)
XLA Ops:
  0.6 23.2 %shard_map.68 = (bf16[4,192,1024]{2,1,0:T(8,128)(2,1)S(1)}, bf16[4096,128]{1,0:T(8,128)(2,1)S(1)}, bf16[2,288,128]{2,1,0:T(8,128)(2,1)S(1)}, bf16[512,512]{1,0:T...) custom-call(bf16[4,64,512]{2,1,0:T(8,128)(2,1)} %lat.1, bf16[4,64,64]{2,1,0:T(8,128)(2,1)} %rot.1, ...), custom_call_target="tpu_custom_call" | custom-call | tf_op jit(solution)/shard_map/pallas_call | solution.py:527
  23.8 1.5 %shard_map.69 = (bf16[4,192,1024]{2,1,0:T(8,128)(2,1)}, bf16[4096,128]{1,0:T(8,128)(2,1)}) custom-call(bf16[4,192,1024]{2,1,0:T(8,128)(2,1)S(1)} %get-tuple-element.10.keys, bf16[4096,128]{1,0:T(8,128)(2,1)S(1)} %get-tuple-element.11.values, bf16[2,288,128]{2,1,0:T(8,128)(2,1)S(1)} %get-tuple-element.12.last, bf16[512,512]{1,0:T(8,128)(2,1)S(1)} %get-tuple-element.13.key_w, ...), custom_call_target="tpu_custom_call" | custom-call | tf_op jit(solution)/shard_map/pallas_call | solution.py:564

commit v4 on v3

--- a/solution.py
+++ b/solution.py
@@ -10,8 +10,8 @@
 MESH = pl.DeviceIdType.MESH
 LANES = 128
 BF16 = jnp.bfloat16
-SHIFT = 1
-HELD = 0
+GIVEN = 4, 18
+HELD = 1
 
 
 def xor(me, step, count):
@@ -92,6 +92,9 @@
     slabs = latent // LANES
     tail = slabs * blk
     half = blk // 2
+    give = stage.shape[1] // 16 * GIVEN[0] // GIVEN[1] * 16
+    keep = stage.shape[1] - give
+    kept, given = pl.ds(0, keep), pl.ds(keep, give)
     ways = mid.shape[0]
     per_unit = LANES // blk
     units = planes // per_unit
@@ -163,14 +166,20 @@
     def own_side(s):
         return remote(stage.at[s], raw.at[c, g], got.at[g, c], {"ctx": s})
 
-    def forward(way, i, to):
-        return remote(mid.at[way % ways, 0, i - 1], mid.at[way % ways, 1, i - 1], mid_got.at[way % ways, 1, i - 1], {"group": to})
-
-    def scatter(way, far, i, p, s):
-        return remote(mid.at[way % ways, far, i - 1], raw.at[c, p], got.at[p, c], {"ctx": s})
+    def forward(way, i, part, to):
+        return remote(
+            mid.at[way % ways, 0, i - 1, part], mid.at[way % ways, 1, i - 1, part],
+            mid_got.at[way % ways, 1, i - 1], {"group": to},
+        )
+
+    def scatter(way, far, i, part, p, s):
+        return remote(mid.at[way % ways, far, i - 1, part], raw.at[c, p, part], got.at[p, c], {"ctx": s})
 
     def relay(p, q, to):
         return remote(raw.at[q, p], raw.at[q, p], got.at[p, q], {"group": to})
+
+    def relay_given(p, q, to):
+        return remote(raw.at[q, p, given], raw.at[q, p, given], got.at[p, q], {"group": to})
 
     whole = pl.ds(0, stage.shape[1])
     wide_part, rot_part = pl.ds(0, tail), pl.ds(tail, half)
@@ -302,22 +311,32 @@
 
         near_first(go)
 
-    def direct(way, far, origin, i):
-        if way == 0 or not SHIFT:
-            return inner(way, far)
-        return inner(way, far) & ((origin > 0) | (i != SHIFT) | (ens > 0))
+    def sized(way, go):
+        if way == 0 or not give:
+            go(whole)
+        else:
+            pl.when(c > 0)(lambda: go(whole))
+            pl.when(c == 0)(lambda: go(kept))
 
     def pass_mid(far, i):
         def go(way):
-            @pl.when(inner(way, far) if far == 1 else direct(way, far, c, i))
-            def _():
-                forward(way, i, g).wait_recv() if far == 2 else out(way, i, c, whole, g).wait_recv()
-                s = partner(c, i, seqs)
-                scatter(way, far - 1, i, plane(way, far), s).start()
+            s = partner(c, i, seqs)
+
+            @pl.when(inner(way, far))
+            def _():
                 if far == 1:
-                    @pl.when(onward(way) & direct(way, 1, c, i))
+                    out(way, i, c, whole, g).wait_recv()
+                    scatter(way, 0, i, whole, plane(way, far), s).start()
+
+                    @pl.when(onward(way))
                     def _():
-                        forward(way, i, towards(way)).start()
+                        sized(way, lambda part: forward(way, i, part, towards(way)).start())
+                else:
+                    def onto(part):
+                        forward(way, i, part, g).wait_recv()
+                        scatter(way, 1, i, part, plane(way, far), s).start()
+
+                    sized(way, onto)
 
         near_first(go)
 
@@ -332,9 +351,14 @@
                 q = source(c, i, seqs)
                 arrived(plane(way, far), q)
 
-                @pl.when(onward(way) & ((far > 1) | jnp.logical_not(direct(way, 1, q, i))))
+                @pl.when(onward(way) & ((far > 1) | jnp.logical_not(inner(way, 1))))
                 def _():
                     relay(plane(way, far), q, towards(way)).start()
+
+                if way == 1 and give:
+                    @pl.when(below & inner(1, 1) & (far == 1) & (q == 0))
+                    def _():
+                        relay_given(plane(way, far), q, g - 1).start()
 
         near_first(go)
 
@@ -421,29 +445,36 @@
 
     along(2)
 
+    def origin(i):
+        return jnp.where(i == 0, c, source(c, jnp.maximum(i, 0), seqs))
+
     @pl.loop(2, max(planes, 3))
     def _(far):
-        @pl.loop(0, seqs)
+        turn = gate & (far == planes - 2)
+
+        @pl.loop(0, seqs + 1)
         def _(i):
             @pl.when((i == 0) & (far > 2))
             def _():
                 along(far)
 
-            turn = gate & (far == planes - 2)
-
             @pl.when(turn & (ens == 1) & (i == max(seqs - HELD, 1)))
             def _():
                 pl.semaphore_wait(ready.at[1], 1)
 
-            @pl.when(i > 0)
+            @pl.when((i > 0) & (i < seqs))
             def _():
                 take(far, i)
 
+            at = jnp.where(edge, i, i - 1)
+
+            @pl.when((at >= 0) & (at < seqs))
+            def _():
+                settle(origin(at), far, far)
+
             @pl.when(turn & (ens == 0) & (i == seqs - 1))
             def _():
                 pl.semaphore_signal(ready.at[1], inc=1, device_id={"ens": 1}, device_id_type=MESH)
-
-            settle(jnp.where(i == 0, c, source(c, i, seqs)), far, far)
 
     last[...] = raw[end_q, pl.ds(end_u * per_unit, per_unit)]
 
@@ -451,14 +482,23 @@
     total = seqs * (ups + downs + g * ups + (planes - 1 - g) * downs)
     spread = sum(jnp.where(inner(way, far), 1, 0) for way in (0, 1) for far in (1, 2))
     total = total + (seqs - 1) * (1 + spread)
-    if SHIFT:
-        here, there = jnp.where(c == 0, 1, 0), jnp.where(c == partner(0, SHIFT, seqs), 1, 0)
-        change = jnp.where(inner(1, 1) & below, there - here, 0) - jnp.where(inner(1, 2), here, 0)
-        total = total + jnp.where(ens == 0, change, 0)
-
-    @pl.loop(0, total)
+    near, next_near = jnp.where(inner(1, 1) & below, 1, 0), jnp.where(inner(1, 2), 1, 0)
+    parts = jnp.where(c == 0, (seqs - 1) * (near + next_near), 0)
+    if not give:
+        parts = 0 * parts
+
+    @pl.loop(0, total - parts)
     def _(_):
         own_along(g).wait_send()
+
+    @pl.loop(0, parts)
+    def _(_):
+        forward(1, 1, kept, g).wait_send()
+
+    if give:
+        @pl.when((c > 0) & (near > 0))
+        def _():
+            relay_given(g, c, g).wait_send()
 
 
 def store(

time: 25.5 us -> 25.1 us (0.984)
  Pallas kernels: 24.7 us -> 24.2 us
    pallas_call x1, Pallas kernels: 23.2 us -> 22.7 us  [per_device(): pl.pallas_call(functools.partial(kernel, seqs, planes, heads, rotary), ou...]
where the time goes in v4:
time: 25.1 us; the launch traced here: 24.9 us
  Pallas kernels  24.2 us (96%)
  between operations  0.64 us (3%)
    pallas_call x1, Pallas kernels, per_device(): pl.pallas_call(functools.partial(kernel, seqs, planes, heads, rotary), ou...  22.7 us
    pallas_call x1, Pallas kernels, per_device(): pl.pallas_call(functools.partial(store, seqs, planes, heads, rotary, blk)...  1.51 us

profile of v4, /device:TPU:0, one launch (start us, length us, event | category | flops | bytes accessed | tf_op | source)
XLA Modules:
  0.0 24.9 jit_solution(15818232718596265718)
XLA Ops:
  0.6 22.7 %shard_map.68 = (bf16[4,192,1024]{2,1,0:T(8,128)(2,1)S(1)}, bf16[4096,128]{1,0:T(8,128)(2,1)S(1)}, bf16[2,288,128]{2,1,0:T(8,128)(2,1)S(1)}, bf16[512,512]{1,0:T...) custom-call(bf16[4,64,512]{2,1,0:T(8,128)(2,1)} %lat.1, bf16[4,64,64]{2,1,0:T(8,128)(2,1)} %rot.1, ...), custom_call_target="tpu_custom_call" | custom-call | tf_op jit(solution)/shard_map/pallas_call | solution.py:567
  23.4 1.5 %shard_map.69 = (bf16[4,192,1024]{2,1,0:T(8,128)(2,1)}, bf16[4096,128]{1,0:T(8,128)(2,1)}) custom-call(bf16[4,192,1024]{2,1,0:T(8,128)(2,1)S(1)} %get-tuple-element.10.keys, bf16[4096,128]{1,0:T(8,128)(2,1)S(1)} %get-tuple-element.11.values, bf16[2,288,128]{2,1,0:T(8,128)(2,1)S(1)} %get-tuple-element.12.last, bf16[512,512]{1,0:T(8,128)(2,1)S(1)} %get-tuple-element.13.key_w, ...), custom_call_target="tpu_custom_call" | custom-call | tf_op jit(solution)/shard_map/pallas_call | solution.py:604

commit v5 on v4

--- a/solution.py
+++ b/solution.py
@@ -10,8 +10,8 @@
 MESH = pl.DeviceIdType.MESH
 LANES = 128
 BF16 = jnp.bfloat16
-GIVEN = 4, 18
-HELD = 1
+GIVEN = 3, 18
+HELD, HELD_FIRST = 2, 1
 
 
 def xor(me, step, count):
@@ -117,12 +117,12 @@
     @pl.loop(1, seqs)
     def _(b):
         for k in range(slabs):
-            lat_load(partner(first, b, seqs), k, 2).start()
+            lat_load(partner(first, b, seqs), k, 0).start()
 
     loads = [
-        pltpu.make_async_copy(key_up, key_stage, load_sem.at[3]),
-        pltpu.make_async_copy(value_up, value_stage, load_sem.at[3]),
-        pltpu.make_async_copy(gain_in, gain, load_sem.at[3]),
+        pltpu.make_async_copy(key_up, key_stage, load_sem.at[2]),
+        pltpu.make_async_copy(value_up, value_stage, load_sem.at[2]),
+        pltpu.make_async_copy(gain_in, gain, load_sem.at[2]),
     ]
     for load in loads:
         load.start()
@@ -130,7 +130,7 @@
     barrier = pltpu.get_barrier_semaphore()
     above, below = g < planes - 1, g > 0
     edge = (g == 0) | (g == planes - 1)
-    gate = (g == 1) | (g == planes - 2) if planes > 3 and HELD else g < 0
+    gate = (g == 1) | (g == planes - 2) if planes > 3 else g < 0
 
     def inner(way, far):
         return g > far if way == 0 else g + far < planes - 1
@@ -203,7 +203,7 @@
     def _(s):
         @pl.when(join(c, s, seqs) == c)
         def _():
-            pl.semaphore_signal(ready.at[2 + c], inc=1, device_id={"ctx": s}, device_id_type=MESH)
+            pl.semaphore_signal(ready.at[1 + c], inc=1, device_id={"ctx": s}, device_id_type=MESH)
 
     def prepare():
         for load in loads:
@@ -226,6 +226,11 @@
     def _():
         out(1, 1, first, wide_part, g - 1).start()
 
+    @pl.loop(1, seqs)
+    def _(b):
+        for k in range(slabs):
+            lat_load(partner(first, b, seqs), k, 0).wait()
+
     rot_load.wait()
 
     @pl.loop(0, seqs)
@@ -233,11 +238,6 @@
         block = rot_stage[s].astype(jnp.float32)
         both = jnp.concatenate([block[:half], block[half:]], axis=1)
         stage[s, pl.ds(tail, half), :] = both.astype(BF16)
-
-    @pl.loop(1, seqs)
-    def _(b):
-        for k in range(slabs):
-            lat_load(partner(first, b, seqs), k, 2).wait()
 
     @pl.when(below & above)
     def _():
@@ -264,7 +264,7 @@
         def _():
             @pl.when(t > c)
             def _():
-                pl.semaphore_wait(ready.at[2 + t], 1)
+                pl.semaphore_wait(ready.at[1 + t], 1)
 
             @pl.loop(1, seqs)
             def _(i):
@@ -445,6 +445,31 @@
 
     along(2)
 
+    def drain():
+        ups, downs = jnp.minimum(planes - 1 - g, 1), jnp.minimum(g, 1)
+        total = seqs * (ups + downs + g * ups + (planes - 1 - g) * downs)
+        spread = sum(jnp.where(inner(way, far), 1, 0) for way in (0, 1) for far in (1, 2))
+        total = total + (seqs - 1) * (1 + spread)
+        near, next_near = jnp.where(inner(1, 1) & below, 1, 0), jnp.where(inner(1, 2), 1, 0)
+        parts = jnp.where(c == 0, (seqs - 1) * (near + next_near), 0)
+        if not give:
+            parts = 0 * parts
+
+        @pl.loop(0, total - parts)
+        def _(_):
+            own_along(g).wait_send()
+
+        @pl.loop(0, parts)
+        def _(_):
+            forward(1, 1, kept, g).wait_send()
+
+        if give:
+            @pl.when((c > 0) & (near > 0))
+            def _():
+                relay_given(g, c, g).wait_send()
+
+    pl.when(edge)(drain)
+
     def origin(i):
         return jnp.where(i == 0, c, source(c, jnp.maximum(i, 0), seqs))
 
@@ -458,47 +483,34 @@
             def _():
                 along(far)
 
-            @pl.when(turn & (ens == 1) & (i == max(seqs - HELD, 1)))
+            @pl.when(turn & (ens == 1) & (i == jnp.where(c == 0, seqs - HELD_FIRST, max(seqs - HELD, 1))))
             def _():
                 pl.semaphore_wait(ready.at[1], 1)
 
+            at = jnp.where(edge, i, i - 1)
+            late = turn & (ens == 1) & (i == seqs - 1) & (c == 0)
+            pl.when(late)(lambda: settle(origin(at), far, far))
+
             @pl.when((i > 0) & (i < seqs))
             def _():
                 take(far, i)
 
-            at = jnp.where(edge, i, i - 1)
-
-            @pl.when((at >= 0) & (at < seqs))
+            done = turn & (ens == 0) & (i == seqs - 1)
+
+            def release():
+                pl.semaphore_signal(ready.at[1], inc=1, device_id={"ens": 1}, device_id_type=MESH)
+
+            pl.when(done & (c > 0))(release)
+
+            @pl.when((at >= 0) & (at < seqs) & jnp.logical_not(late))
             def _():
                 settle(origin(at), far, far)
 
-            @pl.when(turn & (ens == 0) & (i == seqs - 1))
-            def _():
-                pl.semaphore_signal(ready.at[1], inc=1, device_id={"ens": 1}, device_id_type=MESH)
+            pl.when(done & (c == 0))(release)
 
     last[...] = raw[end_q, pl.ds(end_u * per_unit, per_unit)]
 
-    ups, downs = jnp.minimum(planes - 1 - g, 1), jnp.minimum(g, 1)
-    total = seqs * (ups + downs + g * ups + (planes - 1 - g) * downs)
-    spread = sum(jnp.where(inner(way, far), 1, 0) for way in (0, 1) for far in (1, 2))
-    total = total + (seqs - 1) * (1 + spread)
-    near, next_near = jnp.where(inner(1, 1) & below, 1, 0), jnp.where(inner(1, 2), 1, 0)
-    parts = jnp.where(c == 0, (seqs - 1) * (near + next_near), 0)
-    if not give:
-        parts = 0 * parts
-
-    @pl.loop(0, total - parts)
-    def _(_):
-        own_along(g).wait_send()
-
-    @pl.loop(0, parts)
-    def _(_):
-        forward(1, 1, kept, g).wait_send()
-
-    if give:
-        @pl.when((c > 0) & (near > 0))
-        def _():
-            relay_given(g, c, g).wait_send()
+    pl.when(jnp.logical_not(edge))(drain)
 
 
 def store(
@@ -585,11 +597,11 @@
             pltpu.VMEM((latent * heads, size), BF16),
             pltpu.VMEM((latent * heads, size), jnp.float32),
             pltpu.VMEM((LANES * heads, size), jnp.float32),
-            dma((4,)),
+            dma((3,)),
             dma((planes, seqs)),
             dma((ways, 2, seqs - 1)),
             dma,
-            pltpu.SemaphoreType.REGULAR((2 + seqs,)),
+            pltpu.SemaphoreType.REGULAR((1 + seqs,)),
         ],
         compiler_params=pltpu.CompilerParams(
             collective_id=0, has_side_effects=True, vmem_limit_bytes=32 * 1024 * 1024

time: 25.1 us -> 24.9 us (level)
  the two profiles are of different devices: /device:TPU:0 before, /device:TPU:3 now
where the time goes in v5:
time: 24.9 us; the launch traced here: 24.7 us
  Pallas kernels  24.1 us (97%)
  between operations  0.64 us (3%)
    pallas_call x1, Pallas kernels, per_device(): pl.pallas_call(functools.partial(kernel, seqs, planes, heads, rotary), ou...  22.6 us
    pallas_call x1, Pallas kernels, per_device(): pl.pallas_call(functools.partial(store, seqs, planes, heads, rotary, blk)...  1.51 us

profile of v5, /device:TPU:3, one launch (start us, length us, event | category | flops | bytes accessed | tf_op | source)
XLA Modules:
  0.0 24.7 jit_solution(8937632563246423140)
XLA Ops:
  0.6 22.6 %shard_map.68 = (bf16[4,192,1024]{2,1,0:T(8,128)(2,1)S(1)}, bf16[4096,128]{1,0:T(8,128)(2,1)S(1)}, bf16[2,288,128]{2,1,0:T(8,128)(2,1)S(1)}, bf16[512,512]{1,0:T...) custom-call(bf16[4,64,512]{2,1,0:T(8,128)(2,1)} %lat.1, bf16[4,64,64]{2,1,0:T(8,128)(2,1)} %rot.1, ...), custom_call_target="tpu_custom_call" | custom-call | tf_op jit(solution)/shard_map/pallas_call | solution.py:579
  23.2 1.5 %shard_map.69 = (bf16[4,192,1024]{2,1,0:T(8,128)(2,1)}, bf16[4096,128]{1,0:T(8,128)(2,1)}) custom-call(bf16[4,192,1024]{2,1,0:T(8,128)(2,1)S(1)} %get-tuple-element.10.keys, bf16[4096,128]{1,0:T(8,128)(2,1)S(1)} %get-tuple-element.11.values, bf16[2,288,128]{2,1,0:T(8,128)(2,1)S(1)} %get-tuple-element.12.last, bf16[512,512]{1,0:T(8,128)(2,1)S(1)} %get-tuple-element.13.key_w, ...), custom_call_target="tpu_custom_call" | custom-call | tf_op jit(solution)/shard_map/pallas_call | solution.py:616

commit v6 on v5

--- a/solution.py
+++ b/solution.py
@@ -11,7 +11,7 @@
 LANES = 128
 BF16 = jnp.bfloat16
 GIVEN = 3, 18
-HELD, HELD_FIRST = 2, 1
+HELD = 1
 
 
 def xor(me, step, count):
@@ -219,12 +219,17 @@
                 wide[pl.ds(h, latent, stride=heads), :].astype(BF16)
             )
 
+    @pl.when(below & above)
+    def _():
+        for k in range(slabs):
+            remote(
+                lat.at[first, :, pl.ds(k * LANES, LANES)],
+                mid.at[1 % ways, 0, 0, pl.ds(k * blk, blk)],
+                mid_got.at[1 % ways, 0, 0], {"group": g - 1},
+            ).start()
+
     for k in range(slabs):
         lat_load(first, k, 1).wait()
-
-    @pl.when(below & above)
-    def _():
-        out(1, 1, first, wide_part, g - 1).start()
 
     @pl.loop(1, seqs)
     def _(b):
@@ -483,7 +488,7 @@
             def _():
                 along(far)
 
-            @pl.when(turn & (ens == 1) & (i == jnp.where(c == 0, seqs - HELD_FIRST, max(seqs - HELD, 1))))
+            @pl.when(turn & (ens == 1) & (i == max(seqs - HELD, 1)))
             def _():
                 pl.semaphore_wait(ready.at[1], 1)
 

time: 24.9 us -> 24.7 us (level)
  the two profiles are of different devices: /device:TPU:3 before, /device:TPU:0 now
where the time goes in v6:
time: 24.7 us; the launch traced here: 24.3 us
  Pallas kernels  23.7 us (96%)
  between operations  0.64 us (3%)
    pallas_call x1, Pallas kernels, per_device(): pl.pallas_call(functools.partial(kernel, seqs, planes, heads, rotary), ou...  22.2 us
    pallas_call x1, Pallas kernels, per_device(): pl.pallas_call(functools.partial(store, seqs, planes, heads, rotary, blk)...  1.51 us

profile of v6, /device:TPU:0, one launch (start us, length us, event | category | flops | bytes accessed | tf_op | source)
XLA Modules:
  0.0 24.3 jit_solution(8673528553728205582)
XLA Ops:
  0.6 22.2 %shard_map.68 = (bf16[4,192,1024]{2,1,0:T(8,128)(2,1)S(1)}, bf16[4096,128]{1,0:T(8,128)(2,1)S(1)}, bf16[2,288,128]{2,1,0:T(8,128)(2,1)S(1)}, bf16[512,512]{1,0:T...) custom-call(bf16[4,64,512]{2,1,0:T(8,128)(2,1)} %lat.1, bf16[4,64,64]{2,1,0:T(8,128)(2,1)} %rot.1, ...), custom_call_target="tpu_custom_call" | custom-call | tf_op jit(solution)/shard_map/pallas_call | solution.py:584
  22.8 1.5 %shard_map.69 = (bf16[4,192,1024]{2,1,0:T(8,128)(2,1)}, bf16[4096,128]{1,0:T(8,128)(2,1)}) custom-call(bf16[4,192,1024]{2,1,0:T(8,128)(2,1)S(1)} %get-tuple-element.10.keys, bf16[4096,128]{1,0:T(8,128)(2,1)S(1)} %get-tuple-element.11.values, bf16[2,288,128]{2,1,0:T(8,128)(2,1)S(1)} %get-tuple-element.12.last, bf16[512,512]{1,0:T(8,128)(2,1)S(1)} %get-tuple-element.13.key_w, ...), custom_call_target="tpu_custom_call" | custom-call | tf_op jit(solution)/shard_map/pallas_call | solution.py:621

commit v7 on v6

--- a/solution.py
+++ b/solution.py
@@ -239,7 +239,8 @@
     rot_load.wait()
 
     @pl.loop(0, seqs)
-    def _(s):
+    def _(b):
+        s = partner(first, b, seqs)
         block = rot_stage[s].astype(jnp.float32)
         both = jnp.concatenate([block[:half], block[half:]], axis=1)
         stage[s, pl.ds(tail, half), :] = both.astype(BF16)

time: 24.7 us -> 24.7 us (level)
  no operation moved by 1% of the time
where the time goes in v7:
time: 24.7 us; the launch traced here: 24.4 us
  Pallas kernels  23.7 us (96%)
  between operations  0.64 us (3%)
    pallas_call x1, Pallas kernels, per_device(): pl.pallas_call(functools.partial(kernel, seqs, planes, heads, rotary), ou...  22.2 us
    pallas_call x1, Pallas kernels, per_device(): pl.pallas_call(functools.partial(store, seqs, planes, heads, rotary, blk)...  1.51 us

profile of v7, /device:TPU:0, one launch (start us, length us, event | category | flops | bytes accessed | tf_op | source)
XLA Modules:
  0.0 24.4 jit_solution(508157791415366371)
XLA Ops:
  0.6 22.2 %shard_map.68 = (bf16[4,192,1024]{2,1,0:T(8,128)(2,1)S(1)}, bf16[4096,128]{1,0:T(8,128)(2,1)S(1)}, bf16[2,288,128]{2,1,0:T(8,128)(2,1)S(1)}, bf16[512,512]{1,0:T...) custom-call(bf16[4,64,512]{2,1,0:T(8,128)(2,1)} %lat.1, bf16[4,64,64]{2,1,0:T(8,128)(2,1)} %rot.1, ...), custom_call_target="tpu_custom_call" | custom-call | tf_op jit(solution)/shard_map/pallas_call | solution.py:585
  22.8 1.5 %shard_map.69 = (bf16[4,192,1024]{2,1,0:T(8,128)(2,1)}, bf16[4096,128]{1,0:T(8,128)(2,1)}) custom-call(bf16[4,192,1024]{2,1,0:T(8,128)(2,1)S(1)} %get-tuple-element.10.keys, bf16[4096,128]{1,0:T(8,128)(2,1)S(1)} %get-tuple-element.11.values, bf16[2,288,128]{2,1,0:T(8,128)(2,1)S(1)} %get-tuple-element.12.last, bf16[512,512]{1,0:T(8,128)(2,1)S(1)} %get-tuple-element.13.key_w, ...), custom_call_target="tpu_custom_call" | custom-call | tf_op jit(solution)/shard_map/pallas_call | solution.py:622

commit v8 on v7

--- a/solution.py
+++ b/solution.py
@@ -10,7 +10,7 @@
 MESH = pl.DeviceIdType.MESH
 LANES = 128
 BF16 = jnp.bfloat16
-GIVEN = 3, 18
+GIVEN = 2, 18
 HELD = 1
 
 

time: 24.7 us -> 24.7 us (level)
  no operation moved by 1% of the time
where the time goes in v8:
time: 24.7 us; the launch traced here: 24.4 us
  Pallas kernels  23.8 us (96%)
  between operations  0.64 us (3%)
    pallas_call x1, Pallas kernels, per_device(): pl.pallas_call(functools.partial(kernel, seqs, planes, heads, rotary), ou...  22.3 us
    pallas_call x1, Pallas kernels, per_device(): pl.pallas_call(functools.partial(store, seqs, planes, heads, rotary, blk)...  1.51 us

profile of v8, /device:TPU:0, one launch (start us, length us, event | category | flops | bytes accessed | tf_op | source)
XLA Modules:
  0.0 24.4 jit_solution(13726923771721493508)
XLA Ops:
  0.6 22.3 %shard_map.68 = (bf16[4,192,1024]{2,1,0:T(8,128)(2,1)S(1)}, bf16[4096,128]{1,0:T(8,128)(2,1)S(1)}, bf16[2,288,128]{2,1,0:T(8,128)(2,1)S(1)}, bf16[512,512]{1,0:T...) custom-call(bf16[4,64,512]{2,1,0:T(8,128)(2,1)} %lat.1, bf16[4,64,64]{2,1,0:T(8,128)(2,1)} %rot.1, ...), custom_call_target="tpu_custom_call" | custom-call | tf_op jit(solution)/shard_map/pallas_call | solution.py:585
  22.9 1.5 %shard_map.69 = (bf16[4,192,1024]{2,1,0:T(8,128)(2,1)}, bf16[4096,128]{1,0:T(8,128)(2,1)}) custom-call(bf16[4,192,1024]{2,1,0:T(8,128)(2,1)S(1)} %get-tuple-element.10.keys, bf16[4096,128]{1,0:T(8,128)(2,1)S(1)} %get-tuple-element.11.values, bf16[2,288,128]{2,1,0:T(8,128)(2,1)S(1)} %get-tuple-element.12.last, bf16[512,512]{1,0:T(8,128)(2,1)S(1)} %get-tuple-element.13.key_w, ...), custom_call_target="tpu_custom_call" | custom-call | tf_op jit(solution)/shard_map/pallas_call | solution.py:622

commit v9 on v8

--- a/solution.py
+++ b/solution.py
@@ -114,6 +114,68 @@
         lat_load(first, k, 1).start()
     rot_load.start()
 
+    barrier = pltpu.get_barrier_semaphore()
+    above, below = g < planes - 1, g > 0
+    edge = (g == 0) | (g == planes - 1)
+    gate = (g == 1) | (g == planes - 2) if planes > 3 else g < 0
+
+    def inner(way, far):
+        return g > far if way == 0 else g + far < planes - 1
+
+    @pl.when(above)
+    def _():
+        pl.semaphore_signal(barrier, inc=1, device_id={"group": g + 1}, device_id_type=MESH)
+
+    @pl.when(gate & (ens == 1))
+    def _():
+        pl.semaphore_signal(barrier, inc=1, device_id={"ens": 0}, device_id_type=MESH)
+
+    @pl.loop(c + 1, seqs)
+    def _(s):
+        @pl.when(join(c, s, seqs) == s)
+        def _():
+            pl.semaphore_signal(barrier, inc=1, device_id={"ctx": s}, device_id_type=MESH)
+
+    def remote(src, dst, in_sem, to):
+        return pltpu.make_async_remote_copy(
+            src_ref=src, dst_ref=dst, send_sem=sent, recv_sem=in_sem,
+            device_id=to, device_id_type=MESH,
+        )
+
+    def out(way, i, s, part, to):
+        return remote(
+            stage.at[s, part], mid.at[way % ways, 0, i - 1, part], mid_got.at[way % ways, 0, i - 1], {"group": to}
+        )
+
+    def own_along(to):
+        return remote(stage.at[c], raw.at[c, g], got.at[g, c], {"group": to})
+
+    def own_side(s):
+        return remote(stage.at[s], raw.at[c, g], got.at[g, c], {"ctx": s})
+
+    def forward(way, i, part, to):
+        return remote(
+            mid.at[way % ways, 0, i - 1, part], mid.at[way % ways, 1, i - 1, part],
+            mid_got.at[way % ways, 1, i - 1], {"group": to},
+        )
+
+    def scatter(way, far, i, part, p, s):
+        return remote(mid.at[way % ways, far, i - 1, part], raw.at[c, p, part], got.at[p, c], {"ctx": s})
+
+    def relay(p, q, to):
+        return remote(raw.at[q, p], raw.at[q, p], got.at[p, q], {"group": to})
+
+    def relay_given(p, q, to):
+        return remote(raw.at[q, p, given], raw.at[q, p, given], got.at[p, q], {"group": to})
+
+    whole = pl.ds(0, stage.shape[1])
+    wide_part, rot_part = pl.ds(0, tail), pl.ds(tail, half)
+
+    def rest(way, to):
+        @pl.loop(2, seqs)
+        def _(i):
+            out(way, i, partner(c, i, seqs), whole, to).start()
+
     @pl.loop(1, seqs)
     def _(b):
         for k in range(slabs):
@@ -126,68 +188,6 @@
     ]
     for load in loads:
         load.start()
-
-    barrier = pltpu.get_barrier_semaphore()
-    above, below = g < planes - 1, g > 0
-    edge = (g == 0) | (g == planes - 1)
-    gate = (g == 1) | (g == planes - 2) if planes > 3 else g < 0
-
-    def inner(way, far):
-        return g > far if way == 0 else g + far < planes - 1
-
-    @pl.when(above)
-    def _():
-        pl.semaphore_signal(barrier, inc=1, device_id={"group": g + 1}, device_id_type=MESH)
-
-    @pl.when(gate & (ens == 1))
-    def _():
-        pl.semaphore_signal(barrier, inc=1, device_id={"ens": 0}, device_id_type=MESH)
-
-    @pl.loop(c + 1, seqs)
-    def _(s):
-        @pl.when(join(c, s, seqs) == s)
-        def _():
-            pl.semaphore_signal(barrier, inc=1, device_id={"ctx": s}, device_id_type=MESH)
-
-    def remote(src, dst, in_sem, to):
-        return pltpu.make_async_remote_copy(
-            src_ref=src, dst_ref=dst, send_sem=sent, recv_sem=in_sem,
-            device_id=to, device_id_type=MESH,
-        )
-
-    def out(way, i, s, part, to):
-        return remote(
-            stage.at[s, part], mid.at[way % ways, 0, i - 1, part], mid_got.at[way % ways, 0, i - 1], {"group": to}
-        )
-
-    def own_along(to):
-        return remote(stage.at[c], raw.at[c, g], got.at[g, c], {"group": to})
-
-    def own_side(s):
-        return remote(stage.at[s], raw.at[c, g], got.at[g, c], {"ctx": s})
-
-    def forward(way, i, part, to):
-        return remote(
-            mid.at[way % ways, 0, i - 1, part], mid.at[way % ways, 1, i - 1, part],
-            mid_got.at[way % ways, 1, i - 1], {"group": to},
-        )
-
-    def scatter(way, far, i, part, p, s):
-        return remote(mid.at[way % ways, far, i - 1, part], raw.at[c, p, part], got.at[p, c], {"ctx": s})
-
-    def relay(p, q, to):
-        return remote(raw.at[q, p], raw.at[q, p], got.at[p, q], {"group": to})
-
-    def relay_given(p, q, to):
-        return remote(raw.at[q, p, given], raw.at[q, p, given], got.at[p, q], {"group": to})
-
-    whole = pl.ds(0, stage.shape[1])
-    wide_part, rot_part = pl.ds(0, tail), pl.ds(tail, half)
-
-    def rest(way, to):
-        @pl.loop(2, seqs)
-        def _(i):
-            out(way, i, partner(c, i, seqs), whole, to).start()
 
     early = lower(c, seqs) + jnp.minimum(g, 1) + jnp.where(gate & (ens == 0), 1, 0)
 

time: 24.7 us -> 24.7 us (level)
  no operation moved by 1% of the time
where the time goes in v9:
time: 24.7 us; the launch traced here: 24.5 us
  Pallas kernels  23.9 us (97%)
  between operations  0.64 us (3%)
    pallas_call x1, Pallas kernels, per_device(): pl.pallas_call(functools.partial(kernel, seqs, planes, heads, rotary), ou...  22.4 us
    pallas_call x1, Pallas kernels, per_device(): pl.pallas_call(functools.partial(store, seqs, planes, heads, rotary, blk)...  1.51 us

profile of v9, /device:TPU:0, one launch (start us, length us, event | category | flops | bytes accessed | tf_op | source)
XLA Modules:
  0.0 24.5 jit_solution(6131989266531417811)
XLA Ops:
  0.6 22.4 %shard_map.68 = (bf16[4,192,1024]{2,1,0:T(8,128)(2,1)S(1)}, bf16[4096,128]{1,0:T(8,128)(2,1)S(1)}, bf16[2,288,128]{2,1,0:T(8,128)(2,1)S(1)}, bf16[512,512]{1,0:T...) custom-call(bf16[4,64,512]{2,1,0:T(8,128)(2,1)} %lat.1, bf16[4,64,64]{2,1,0:T(8,128)(2,1)} %rot.1, ...), custom_call_target="tpu_custom_call" | custom-call | tf_op jit(solution)/shard_map/pallas_call | solution.py:585
  23.0 1.5 %shard_map.69 = (bf16[4,192,1024]{2,1,0:T(8,128)(2,1)}, bf16[4096,128]{1,0:T(8,128)(2,1)}) custom-call(bf16[4,192,1024]{2,1,0:T(8,128)(2,1)S(1)} %get-tuple-element.10.keys, bf16[4096,128]{1,0:T(8,128)(2,1)S(1)} %get-tuple-element.11.values, bf16[2,288,128]{2,1,0:T(8,128)(2,1)S(1)} %get-tuple-element.12.last, bf16[512,512]{1,0:T(8,128)(2,1)S(1)} %get-tuple-element.13.key_w, ...), custom_call_target="tpu_custom_call" | custom-call | tf_op jit(solution)/shard_map/pallas_call | solution.py:622
